TPU v7x, 32 devices: a whole 2x2x4 slice. The times are simulated.
32 devices in a mesh: intra: 4 (over y, x), inter: 8 (over z, core).
Axes of the slice: x: 2, y: 2, z: 4, core: 2. Of those that a mesh axis runs over, the one named last changes fastest.
Arguments:
- acts: bfloat16 [4096, 4096], P(('intra', 'inter')), may hold values from -6 to 6
- grad_out: bfloat16 [4096, 512], P(('intra', 'inter')), may hold values from -6 to 6
- codes: int32 [4096, 512], P('intra'), may hold values from -127 to 127
- scales: float32 [2048], P('intra'), may hold values from 0.0002 to 0.0008
Outputs:
- grad_in: bfloat16 [4096, 4096], P(('intra', 'inter'))
- grad_w: float32 [4096, 512], P(('intra', 'inter'))
All inputs are finite; a program needn't handle non-finite values.
Results may differ from a plain program's by a relative error of at most 0.0049.
Values may be sent and summed in bfloat16 or wider, within the bound.
A program may use at most 64 MiB of HBM per device.

v0:
```python
import math
import jax
import jax.numpy as jnp
from jax import lax
from jax.sharding import PartitionSpec as P


def per_device(acts, grad_out, codes, scales):
    rows = codes.shape[0]
    width_kv = codes.shape[1]
    blocks = codes.astype(jnp.float32).reshape(rows // 2, 2 * width_kv) * scales[:, None]
    local_weight = blocks.reshape(rows, width_kv).astype(jnp.bfloat16)
    n_group = lax.axis_size("intra")
    n_cross = lax.axis_size("inter")
    tok_rows = acts.shape[0]
    factor = 1.0 / math.sqrt(tok_rows * n_group * n_cross)
    contract = (((0,), (0,)), ((), ()))
    group_cot = lax.all_gather(grad_out, "intra", axis=0, tiled=True)
    columns_owned = lax.all_to_all(acts, "intra", split_axis=1, concat_axis=0, tiled=True)
    grad_w = lax.psum_scatter(
        lax.dot_general(columns_owned, group_cot, contract, preferred_element_type=jnp.float32)
        * factor,
        "inter",
        scatter_dimension=0,
        tiled=True,
    )
    pieces = jnp.dot(group_cot, local_weight.T, preferred_element_type=jnp.float32).astype(
        jnp.bfloat16
    )
    grad_in = lax.all_to_all(pieces, "intra", split_axis=0, concat_axis=1, tiled=True)
    return (grad_in, grad_w)


def solution(mesh):
    in_specs = (
        P(("intra", "inter"), None),
        P(("intra", "inter"), None),
        P("intra", None),
        P("intra"),
    )
    out_specs = (P(("intra", "inter"), None), P(("intra", "inter"), None))
    return jax.shard_map(
        per_device, mesh=mesh, in_specs=in_specs, out_specs=out_specs, check_vma=False
    )
```

profile of v0, /device:TPU:0, one launch (start us, length us, event | category | flops | bytes accessed | tf_op | source)
XLA Modules:
  0.0 80.3 jit_solution(17842315218123064964)
XLA Ops:
  7.2 0.0 copy-start.1
  7.2 2.3 %copy.9 = bf16[128,4096]{0,1:T(8,128)(2,1)} copy(bf16[128,4096]{1,0:T(8,128)(2,1)} %param.4) | data formatting | bytes 2097152 | tf_op args[0]
  9.5 5.2 %all-to-all-start.1 = ((bf16[128,4,1024]{0,2,1:T(8,128)(2,1)}), bf16[128,4,1024]{0,2,1:T(8,128)(2,1)S(1)}, u32[]{:S(2)}, u32[]{:S(2)}) async-start(bf16[128,4,1024]{0,2,1:T(8,128)(2,1)} %bitcast.3), calls=%async_computation.1 | async-start | bytes 2097152 | tf_op jit(solution)/shard_map/all_to_all | solution.py:19
  14.7 0.0 reduce-scatter.2.cloned.1.call-start
  14.7 0.0 copy-done.1
  14.7 19.4 %all_gather.3 = bf16[512,512]{1,0:T(8,128)(2,1)S(1)} all-gather(bf16[128,512]{1,0:T(8,128)(2,1)S(1)} %copy-done.1), channel_id=1, replica_groups=mesh['intra'=4,'inter'=8] {'intra'}, dimensions={0}, use_global_device_ids=true | all-gather | bytes 655360 | tf_op jit(solution)/shard_map/all_gather | solution.py:18
  34.1 0.0 all-to-all-done.1
  34.1 0.5 copy.10
  34.7 0.0 copy-start.2
  34.7 2.1 %convolution_multiply_fusion = f32[1024,512]{1,0:T(8,128)} fusion(bf16[512,1024]{1,0:T(8,128)(2,1)S(1)} %bitcast.12, bf16[512,512]{1,0:T(8,128)(2,1)S(1)} %all_gather.3), kind=kOutput, calls=%fused_computation.1 | convolution fusion | flops 537395200 | bytes 3670016 | tf_op jit(solution)/shard_map/dot_general | solution.py:21
  36.8 0.0 copy-start
  36.8 0.0 reduce-scatter.2.cloned.1.call-update
  36.8 0.0 copy-done.2
  36.8 0.1 mul.19
  36.9 0.2 mul.20
  37.1 1.3 %copy-done = s32[1024,512]{1,0:T(8,128)S(1)} copy-done((s32[1024,512]{1,0:T(8,128)S(1)}, s32[1024,512]{1,0:T(8,128)}, u32[]{:S(2)}) %copy-start) | copy-done | bytes 2097176
  38.4 0.8 %convolution_convert_fusion = bf16[1024,512]{0,1:T(8,128)(2,1)S(1)} fusion(bf16[512,512]{1,0:T(8,128)(2,1)S(1)} %all_gather.3, s32[1024,512]{1,0:T(8,128)S(1)} %copy-done, f32[1024]{0:T(1024)S(1)} %mul.20), kind=kOutput, calls=%fused_computation.2 | convolution fusion | flops 538968064 | bytes 3674112 | tf_op jit(solution)/shard_map/dot_general | solution.py:27
  39.2 14.9 %all_to_all.38 = bf16[4,128,1024]{2,1,0:T(8,128)(2,1)S(1)} all-to-all(bf16[4,128,1024]{2,1,0:T(8,128)(2,1)S(1)} %bitcast.15), channel_id=1, replica_groups=mesh['intra'=4,'inter'=8] {'intra'}, dimensions={0} | all-to-all | bytes 2097152 | tf_op jit(solution)/shard_map/all_to_all | solution.py:30
  54.1 1.1 %copy.11 = bf16[4,16,8,1024]{3,2,0,1:T(8,128)(2,1)} copy(bf16[4,16,8,1024]{3,2,1,0:T(8,128)(2,1)S(1)} %bitcast.14) | data formatting | bytes 2097152 | tf_op jit(solution)/shard_map/all_to_all | solution.py:30
  55.1 18.4 %reduce-scatter.2.cloned.1.call-done = f32[128,512]{1,0:T(8,128)} async-done(((f32[1024,512]{1,0:T(8,128)}), f32[128,512]{1,0:T(8,128)}) %reduce-scatter.2.cloned.1.call-update) | async-done | bytes 262160 | tf_op jit(solution)/shard_map/reduce_scatter | solution.py:20
Async XLA Ops:
  7.2 7.5 %copy-start.1 = (bf16[128,512]{1,0:T(8,128)(2,1)S(1)}, bf16[128,512]{1,0:T(8,128)(2,1)}, u32[]{:S(2)}) copy-start(bf16[128,512]{1,0:T(8,128)(2,1)} %param.5) | copy-start | bytes 393220
  9.5 24.6 %all-to-all-start.1 = ((bf16[128,4,1024]{0,2,1:T(8,128)(2,1)}), bf16[128,4,1024]{0,2,1:T(8,128)(2,1)S(1)}, u32[]{:S(2)}, u32[]{:S(2)}) async-start(bf16[128,4,1024]{0,2,1:T(8,128)(2,1)} %bitcast.3), calls=%async_computation.1 | async-start | bytes 2097152 | tf_op jit(solution)/shard_map/all_to_all | solution.py:19
  14.7 58.8 %reduce-scatter.2.cloned.1.call-start = ((), (), s32[]{:S(2)}) async-start(), calls=%async_computation.3 | async-start | bytes 2359296 | tf_op jit(solution)/shard_map/reduce_scatter | solution.py:20
  34.7 2.1 %copy-start.2 = (f32[512]{0:T(512)S(1)}, f32[512]{0:T(512)}, u32[]{:S(2)}) copy-start(f32[512]{0:T(512)} %param.7) | copy-start | bytes 6148
  36.8 1.6 %copy-start = (s32[1024,512]{1,0:T(8,128)S(1)}, s32[1024,512]{1,0:T(8,128)}, u32[]{:S(2)}) copy-start(s32[1024,512]{1,0:T(8,128)} %param.6) | copy-start | bytes 6291460
Sparse Core Ops, SparseCore 0:
  36.9 36.5 reduce-scatter.1
where the time goes:
time: 80.6 us; the launch traced here: 80.3 us
  blocking collectives  34.3 us (43%)
  waiting for transfers between devices  18.4 us (23%)
  between operations  14.1 us (17%)
  local copies, waits for them, and re-layouts  5.45 us (7%)
  starting transfers between devices  5.19 us (6%)
  matrix products  2.93 us (4%)
    all_gather x1, blocking collectives, per_device(): group_cot = lax.all_gather(grad_out, 'intra', axis=0, tiled=True)  19.4 us
    reduce_scatter x1, waiting for transfers between devices, per_device(): lax.psum_scatter(lax.dot_general(columns_owned, group_cot, contract, pref...  18.4 us
    all_to_all x1, blocking collectives, per_device(): lax.all_to_all(pieces, 'intra', split_axis=0, concat_axis=1, tiled=True)  14.9 us
    all_to_all x1, starting transfers between devices, per_device(): lax.all_to_all(acts, 'intra', split_axis=1, concat_axis=0, tiled=True)  5.19 us
    unnamed x7, local copies, waits for them, and re-layouts  3.56 us
    dot_general x1, matrix products, per_device(): lax.dot_general(columns_owned, group_cot, contract, preferred_element_typ...  2.09 us
  transfers between devices with their start and end apart: 2, of which 1 were waited for; matrix products, arithmetic and copies ran while one was open for 3% of the time, Pallas kernels for 0%

commit v1 on v0

--- a/solution.py
+++ b/solution.py
@@ -15,7 +15,14 @@
     tok_rows = acts.shape[0]
     factor = 1.0 / math.sqrt(tok_rows * n_group * n_cross)
     contract = (((0,), (0,)), ((), ()))
-    group_cot = lax.all_gather(grad_out, "intra", axis=0, tiled=True)
+    ring = [grad_out]
+    for hop in range(3):
+        ring.append(lax.ppermute(ring[-1], "intra", [(dev, (dev + 1) % 4) for dev in range(4)]))
+    group_cot = jnp.roll(
+        jnp.concatenate(ring[::-1], axis=0),
+        (lax.axis_index("intra") + 1) * ring[0].shape[0],
+        axis=0,
+    )
     columns_owned = lax.all_to_all(acts, "intra", split_axis=1, concat_axis=0, tiled=True)
     grad_w = lax.psum_scatter(
         lax.dot_general(columns_owned, group_cot, contract, preferred_element_type=jnp.float32)

time: 80.6 us -> 87.6 us (1.087)
  waiting for transfers between devices: 18.4 us -> 39.3 us
  blocking collectives: 34.3 us -> 15.4 us
  starting transfers between devices: 5.19 us -> 8.23 us
  local copies, waits for them, and re-layouts: 5.45 us -> 7.3 us
    all_gather x1 -> x0, blocking collectives: 19.4 us -> none  [per_device(): group_cot = lax.all_gather(grad_out, 'intra', axis=0, tiled=True)]
    all_to_all x1, waiting for transfers between devices: 0.01 us -> 11.9 us  [per_device(): lax.all_to_all(acts, 'intra', split_axis=1, concat_axis=0, tiled=True)]
    ppermute x0 -> x3, waiting for transfers between devices: none -> 9.77 us  [per_device(): lax.ppermute(ring[-1], 'intra', [(dev, (dev + 1) % 4) for dev in range(4)])]
    ppermute x0 -> x3, starting transfers between devices: none -> 3.8 us  [per_device(): lax.ppermute(ring[-1], 'intra', [(dev, (dev + 1) % 4) for dev in range(4)])]
    unnamed x7 -> x15, local copies, waits for them, and re-layouts: 3.56 us -> 5.41 us
  transfers between devices with their start and end apart: 2 -> 5, of which waited for: 1 -> 4; matrix products, arithmetic and copies ran while one was open for 3% -> 5% of each run, Pallas kernels for 0% -> 0%
where the time goes in v1:
time: 87.6 us; the launch traced here: 87.3 us
  waiting for transfers between devices  39.3 us (45%)
  blocking collectives  15.4 us (18%)
  between operations  14.1 us (16%)
  starting transfers between devices  8.23 us (9%)
  local copies, waits for them, and re-layouts  7.3 us (8%)
  matrix products  2.92 us (3%)
    reduce_scatter x1, waiting for transfers between devices, per_device(): lax.psum_scatter(lax.dot_general(columns_owned, group_cot, contract, pref...  17.6 us
    all_to_all x1, blocking collectives, per_device(): lax.all_to_all(pieces, 'intra', split_axis=0, concat_axis=1, tiled=True)  15.4 us
    all_to_all x1, waiting for transfers between devices, per_device(): lax.all_to_all(acts, 'intra', split_axis=1, concat_axis=0, tiled=True)  11.9 us
    ppermute x3, waiting for transfers between devices, per_device(): lax.ppermute(ring[-1], 'intra', [(dev, (dev + 1) % 4) for dev in range(4)])  9.77 us
    unnamed x15, local copies, waits for them, and re-layouts  5.41 us
    all_to_all x1, starting transfers between devices, per_device(): lax.all_to_all(acts, 'intra', split_axis=1, concat_axis=0, tiled=True)  4.43 us
    ppermute x3, starting transfers between devices, per_device(): lax.ppermute(ring[-1], 'intra', [(dev, (dev + 1) % 4) for dev in range(4)])  3.8 us
    dot_general x1, matrix products, per_device(): lax.dot_general(columns_owned, group_cot, contract, preferred_element_typ...  2.08 us
  transfers between devices with their start and end apart: 5, of which 4 were waited for; matrix products, arithmetic and copies ran while one was open for 5% of the time, Pallas kernels for 0%

profile of v1, /device:TPU:0, one launch (start us, length us, event | category | flops | bytes accessed | tf_op | source)
XLA Modules:
  0.0 87.3 jit_solution(4097701315883568846)
XLA Ops:
  7.2 0.0 copy-start.1
  7.2 3.0 %collective-permute-start = (bf16[128,512]{1,0:T(8,128)(2,1)}, bf16[128,512]{1,0:T(8,128)(2,1)S(1)}, u32[]{:S(2)}, u32[]{:S(2)}) collective-permute-start(bf16[128,512]{1,0:T(8,128)(2,1)} %param.5), channel_id=1, source_target_pairs={{0,8},{8,16},{16,24},{24,0},{1,9},{9,17},{17,25},{25,1},{2,10},{10... | collective-permute-start | bytes 393224 | tf_op jit(solution)/shard_map/ppermute | solution.py:20
  10.2 4.7 %collective-permute-done = bf16[128,512]{1,0:T(8,128)(2,1)S(1)} collective-permute-done((bf16[128,512]{1,0:T(8,128)(2,1)}, bf16[128,512]{1,0:T(8,128)(2,1)S(1)}, u32[]{:S(2)}, u32[]{:S(2)}) %collective-permute-start) | collective-permute-done | bytes 131104 | tf_op jit(solution)/shard_map/ppermute | solution.py:20
  14.9 0.8 collective-permute-start.1
  15.6 5.1 %collective-permute-done.1 = bf16[128,512]{1,0:T(8,128)(2,1)S(1)} collective-permute-done((bf16[128,512]{1,0:T(8,128)(2,1)S(1)}, bf16[128,512]{1,0:T(8,128)(2,1)S(1)}, u32[]{:S(2)}, u32[]{:S(2)}) %collective-permute-start.1) | collective-permute-done | bytes 131104 | tf_op jit(solution)/shard_map/ppermute | solution.py:20
  20.7 0.0 collective-permute-start.2
  20.7 2.3 %copy.11 = bf16[128,4096]{0,1:T(8,128)(2,1)} copy(bf16[128,4096]{1,0:T(8,128)(2,1)} %param.4) | data formatting | bytes 2097152 | tf_op args[0]
  23.0 4.4 %all-to-all-start.1 = ((bf16[128,4,1024]{0,2,1:T(8,128)(2,1)}), bf16[128,4,1024]{0,2,1:T(8,128)(2,1)S(1)}, u32[]{:S(2)}, u32[]{:S(2)}) async-start(bf16[128,4,1024]{0,2,1:T(8,128)(2,1)} %bitcast.2), calls=%async_computation.1 | async-start | bytes 2097152 | tf_op jit(solution)/shard_map/all_to_all | solution.py:26
  27.4 0.0 reduce-scatter.2.cloned.1.call-start
  27.4 0.0 collective-permute-done.2
  27.5 0.0 copy-done.1
  27.6 11.9 %all-to-all-done.1 = bf16[128,4,1024]{0,2,1:T(8,128)(2,1)S(1)} async-done(((bf16[128,4,1024]{0,2,1:T(8,128)(2,1)}), bf16[128,4,1024]{0,2,1:T(8,128)(2,1)S(1)}, u32[]{:S(2)}, u32[]{:S(2)}) %all-to-all-start.1) | async-done | bytes 1048608 | tf_op jit(solution)/shard_map/all_to_all | solution.py:26
  39.5 0.5 copy.12
  40.1 2.1 %multiply_bitcast_fusion = f32[1024,512]{0,1:T(8,128)} fusion(bf16[512,1024]{1,0:T(8,128)(2,1)S(1)} %bitcast.11, bf16[1024,512]{1,0:T(8,128)(2,1)S(1)} %constant_dynamic-update-slice_fusion, s32[]{:T(128)S(6)} %select_n.14), kind=kOutput, calls=%fused_computation | convolution fusion | flops 537395200 | bytes 3670020 | tf_op jit(solution)/shard_map/dot_general | solution.py:28
  42.1 0.0 copy-start.2
  42.2 0.0 copy-start
  42.2 0.0 reduce-scatter.2.cloned.1.call-update
  42.2 0.7 copy-done.2
  42.8 0.1 mul.26
  43.0 0.2 mul.27
  43.1 0.6 copy-done
  43.8 0.8 convolution_convert_fusion
  44.6 15.4 %all_to_all.38 = bf16[4,128,1024]{2,1,0:T(8,128)(2,1)S(1)} all-to-all(bf16[4,128,1024]{2,1,0:T(8,128)(2,1)S(1)} %bitcast.10), channel_id=1, replica_groups=mesh['intra'=4,'inter'=8] {'intra'}, dimensions={0} | all-to-all | bytes 2097152 | tf_op jit(solution)/shard_map/all_to_all | solution.py:37
  60.0 1.1 %copy.14 = bf16[4,16,8,1024]{3,2,0,1:T(8,128)(2,1)} copy(bf16[4,16,8,1024]{3,2,1,0:T(8,128)(2,1)S(1)} %bitcast.13) | data formatting | bytes 2097152 | tf_op jit(solution)/shard_map/all_to_all | solution.py:37
  61.0 17.6 %reduce-scatter.2.cloned.1.call-done = f32[128,512]{0,1:T(8,128)} async-done(((f32[1024,512]{0,1:T(8,128)}), f32[128,512]{0,1:T(8,128)}) %reduce-scatter.2.cloned.1.call-update) | async-done | bytes 262160 | tf_op jit(solution)/shard_map/reduce_scatter | solution.py:27
  78.7 1.8 %copy.13 = f32[128,512]{1,0:T(8,128)} copy(f32[128,512]{0,1:T(8,128)} %reduce-scatter.2.cloned.1.call-done) | data formatting | bytes 524288
  (8 shorter events, 0.1 us)
Async XLA Ops:
  7.2 20.3 %copy-start.1 = (bf16[128,512]{1,0:T(8,128)(2,1)S(1)}, bf16[128,512]{1,0:T(8,128)(2,1)}, u32[]{:S(2)}) copy-start(bf16[128,512]{1,0:T(8,128)(2,1)} %param.5) | copy-start | bytes 393220
  7.2 7.7 %collective-permute-start = (bf16[128,512]{1,0:T(8,128)(2,1)}, bf16[128,512]{1,0:T(8,128)(2,1)S(1)}, u32[]{:S(2)}, u32[]{:S(2)}) collective-permute-start(bf16[128,512]{1,0:T(8,128)(2,1)} %param.5), channel_id=1, source_target_pairs={{0,8},{8,16},{16,24},{24,0},{1,9},{9,17},{17,25},{25,1},{2,10},{10... | collective-permute-start | bytes 393224 | tf_op jit(solution)/shard_map/ppermute | solution.py:20
  14.9 5.9 %collective-permute-start.1 = (bf16[128,512]{1,0:T(8,128)(2,1)S(1)}, bf16[128,512]{1,0:T(8,128)(2,1)S(1)}, u32[]{:S(2)}, u32[]{:S(2)}) collective-permute-start(bf16[128,512]{1,0:T(8,128)(2,1)S(1)} %collective-permute-done), channel_id=1, source_target_pairs={{0,8},{8,16},{16,24},{24,0},{1,9},{9,17},{17,25},{25,1},{2,10},{10... | collective-permute-start | bytes 393224 | tf_op jit(solution)/shard_map/ppermute | solution.py:20
  20.7 6.7 %collective-permute-start.2 = (bf16[128,512]{1,0:T(8,128)(2,1)S(1)}, bf16[128,512]{1,0:T(8,128)(2,1)S(1)}, u32[]{:S(2)}, u32[]{:S(2)}) collective-permute-start(bf16[128,512]{1,0:T(8,128)(2,1)S(1)} %collective-permute-done.1), channel_id=1, source_target_pairs={{0,8},{8,16},{16,24},{24,0},{1,9},{9,17},{17,25},{25,1},{2,10},{10... | collective-permute-start | bytes 393224 | tf_op jit(solution)/shard_map/ppermute | solution.py:20
  23.0 16.5 %all-to-all-start.1 = ((bf16[128,4,1024]{0,2,1:T(8,128)(2,1)}), bf16[128,4,1024]{0,2,1:T(8,128)(2,1)S(1)}, u32[]{:S(2)}, u32[]{:S(2)}) async-start(bf16[128,4,1024]{0,2,1:T(8,128)(2,1)} %bitcast.2), calls=%async_computation.1 | async-start | bytes 2097152 | tf_op jit(solution)/shard_map/all_to_all | solution.py:26
  27.4 51.2 %reduce-scatter.2.cloned.1.call-start = ((), (), s32[]{:S(2)}) async-start(), calls=%async_computation.3 | async-start | bytes 2359296 | tf_op jit(solution)/shard_map/reduce_scatter | solution.py:27
  42.1 0.7 copy-start.2
  42.2 1.6 %copy-start = (s32[1024,512]{1,0:T(8,128)S(1)}, s32[1024,512]{1,0:T(8,128)}, u32[]{:S(2)}) copy-start(s32[1024,512]{1,0:T(8,128)} %param.6) | copy-start | bytes 6291460
Sparse Core Ops, SparseCore 0:
  42.3 36.3 reduce-scatter.1
